TPU v7x, 32 devices: a whole 2x2x4 slice. The times are simulated.
32 devices in a mesh: gx: 4 (over z), gy: 8 (over y, x, core).
Axes of the slice: x: 2, y: 2, z: 4, core: 2. Of those that a mesh axis runs over, the one named last changes fastest.
Arguments:
- greens: bfloat16 [32, 125, 250], P('gy'), may hold values from -6 to 7
- chol_rot: bfloat16 [896, 125, 250], P(('gx', 'gy')), may hold values from -0.0024414062 to 0.0024414062
- one_body: float32 [125, 250], replicated, may hold values from -1 to 1
- weights: float32 [32], P('gy'), may hold values from 0.1 to 10
Outputs:
- local_energy: float32 [32], P('gy')
- mean_energy: float32 [], replicated
All inputs are finite; a program needn't handle non-finite values.
Results may differ from a plain program's by a relative error of at most 0.0003.
Values may be sent and summed in bfloat16 or wider, within the bound.
A program may use at most 256 MiB of HBM per device.

v0:
```python
import math

import jax
import jax.numpy as jnp
from jax import lax
from jax.sharding import PartitionSpec as P

WALK_DEV = 4


def pair_energy(green_block, vector_block):
    walkers = green_block.shape[0]
    vectors = vector_block.shape[0]
    occ = green_block.shape[1]
    orb = green_block.shape[2]
    coulomb = jnp.einsum(
        "wk,gk->wg",
        green_block.reshape(walkers, occ * orb),
        vector_block.reshape(vectors, occ * orb),
        preferred_element_type=jnp.float32,
    )
    exchange = jnp.einsum(
        "ap,bp->ab",
        green_block.reshape(walkers * occ, orb),
        vector_block.reshape(vectors * occ, orb),
        preferred_element_type=jnp.float32,
    )
    exchange = exchange.reshape(walkers, occ, vectors, occ)
    swapped = jnp.transpose(exchange, (0, 3, 2, 1))
    return 0.5 * jnp.sum(coulomb * coulomb, axis=1) - 0.5 * jnp.sum(
        exchange * swapped, axis=(1, 2, 3)
    )


def walker_terms(greens, vectors):
    count = greens.shape[0]
    block = math.gcd(count, WALK_DEV)
    stacked = greens.reshape(count // block, block, greens.shape[1], greens.shape[2])
    parts = lax.map(lambda green_block: pair_energy(green_block, vectors), stacked)
    return parts.reshape(count)


def shards(greens, chol_rot, one_body, weights):
    group_terms = walker_terms(lax.all_gather(greens, "gy", axis=0, tiled=True), chol_rot)
    partial_value = lax.psum_scatter(group_terms, "gy", scatter_dimension=0, tiled=True)
    single = jnp.sum(greens.astype(jnp.float32) * one_body[None, :, :], axis=(1, 2))
    two_body = lax.psum(partial_value, "gx")
    local_energy = single + two_body
    weighted_sum, weight_sum = lax.psum((jnp.sum(weights * local_energy), jnp.sum(weights)), "gy")
    mean_energy = weighted_sum / weight_sum
    return (local_energy, mean_energy)


def solution(mesh):
    placed = (P("gy", None, None), P(("gx", "gy"), None, None), P(), P("gy"))
    return jax.shard_map(
        shards, mesh=mesh, in_specs=placed, out_specs=(P("gy"), P()), check_vma=False
    )
```

profile of v0, /device:TPU:0, one launch (start us, length us, event | category | flops | bytes accessed | tf_op | source)
XLA Modules:
  0.0 300.3 jit_solution(5972364984019195105)
XLA Ops:
  10.8 29.6 %all-gather.2.cloned.1.call-done = bf16[32,125,250]{2,1,0:T(8,128)(2,1)} async-done(((bf16[4,125,250]{2,1,0:T(8,128)(2,1)}), bf16[32,125,250]{2,1,0:T(8,128)(2,1)}) %all-gather.2.cloned.1.call-update) | async-done | bytes 2000016 | tf_op jit(solution)/shard_map/all_gather | solution.py:44
  40.4 211.7 %while.10 = (s32[]{:T(128)}, f32[8,4]{1,0:T(8,128)S(1)}, bf16[8,4,125,250]{3,2,1,0:T(8,128)(2,1)}, bf16[28,125,250]{2,1,0:T(8,128)(2,1)}, s32[]{:T(128)}, /*index=5*/s32[]{:T(128)}) while((s32[]{:T(128)}, f32[8,4]{1,0:T(8,128)S(1)}, bf16[8,4,125,250]{3,2,1,0:T(8,128)(2,1)}, bf16[28,125,250]{2,1,0:T(8,128)(2,1)}, s32[]{:T(128)}, ...), condition=%wide.region_4.5_spmd, body=%wide.region_1.4_spmd.sunk | while | flops 885500160 | bytes 50500224 | solution.py:39
  42.0 4.4 %reshape.56 = bf16[28,31250]{1,0:T(8,128)(2,1)S(1)} reshape(bf16[28,125,250]{2,1,0:T(8,128)(2,1)} %get-tuple-element.78) | data formatting | bytes 3500000 | tf_op jit(solution)/shard_map/while/body/eval_jaxpr/reshape | solution.py:19
  47.8 4.1 %fusion.19 = f32[4,125,28,125]{3,1,2,0:T(8,128)} fusion(bf16[28,125,250]{2,1,0:T(8,128)(2,1)S(1)} %copy-done, bf16[1,4,125,250]{3,2,1,0:T(8,128)(2,1)S(1)} %constant_dynamic-slice_fusion.2), kind=kOutput, calls=%fused_computation.2.clone.1 | convolution fusion | flops 875000000 | bytes 9000000 | tf_op jit(solution)/shard_map/while/body/eval_jaxpr/ap,bp->ab/dot_general | solution.py:22
  52.0 8.5 %copy.14 = f32[4,125,28,125]{1,3,2,0:T(8,128)} copy(f32[4,125,28,125]{3,1,2,0:T(8,128)} %fusion.19) | data formatting | bytes 14000000 | tf_op jit(solution)/shard_map/while/body/eval_jaxpr/ap,bp->ab/dot_general | solution.py:22
  60.5 6.3 %fusion.20 = f32[4]{0:T(128)S(1)} fusion(f32[4,125,28,125]{3,1,2,0:T(8,128)} %fusion.19, f32[4,125,28,125]{1,3,2,0:T(8,128)} %copy.14), kind=kLoop, calls=%fused_computation.1.clone.1 | loop fusion | flops 3499996 | bytes 14000016 | tf_op jit(solution)/shard_map/while/body/eval_jaxpr/reduce_sum | solution.py:30
  68.4 4.4 %reshape.56 = bf16[28,31250]{1,0:T(8,128)(2,1)S(1)} reshape(bf16[28,125,250]{2,1,0:T(8,128)(2,1)} %get-tuple-element.78) | data formatting | bytes 3500000 | tf_op jit(solution)/shard_map/while/body/eval_jaxpr/reshape | solution.py:19
  74.3 4.1 %fusion.19 = f32[4,125,28,125]{3,1,2,0:T(8,128)} fusion(bf16[28,125,250]{2,1,0:T(8,128)(2,1)S(1)} %copy-done, bf16[1,4,125,250]{3,2,1,0:T(8,128)(2,1)S(1)} %constant_dynamic-slice_fusion.2), kind=kOutput, calls=%fused_computation.2.clone.1 | convolution fusion | flops 875000000 | bytes 9000000 | tf_op jit(solution)/shard_map/while/body/eval_jaxpr/ap,bp->ab/dot_general | solution.py:22
  78.4 8.5 %copy.14 = f32[4,125,28,125]{1,3,2,0:T(8,128)} copy(f32[4,125,28,125]{3,1,2,0:T(8,128)} %fusion.19) | data formatting | bytes 14000000 | tf_op jit(solution)/shard_map/while/body/eval_jaxpr/ap,bp->ab/dot_general | solution.py:22
  87.0 6.3 %fusion.20 = f32[4]{0:T(128)S(1)} fusion(f32[4,125,28,125]{3,1,2,0:T(8,128)} %fusion.19, f32[4,125,28,125]{1,3,2,0:T(8,128)} %copy.14), kind=kLoop, calls=%fused_computation.1.clone.1 | loop fusion | flops 3499996 | bytes 14000016 | tf_op jit(solution)/shard_map/while/body/eval_jaxpr/reduce_sum | solution.py:30
  94.9 4.4 %reshape.56 = bf16[28,31250]{1,0:T(8,128)(2,1)S(1)} reshape(bf16[28,125,250]{2,1,0:T(8,128)(2,1)} %get-tuple-element.78) | data formatting | bytes 3500000 | tf_op jit(solution)/shard_map/while/body/eval_jaxpr/reshape | solution.py:19
  100.8 4.1 %fusion.19 = f32[4,125,28,125]{3,1,2,0:T(8,128)} fusion(bf16[28,125,250]{2,1,0:T(8,128)(2,1)S(1)} %copy-done, bf16[1,4,125,250]{3,2,1,0:T(8,128)(2,1)S(1)} %constant_dynamic-slice_fusion.2), kind=kOutput, calls=%fused_computation.2.clone.1 | convolution fusion | flops 875000000 | bytes 9000000 | tf_op jit(solution)/shard_map/while/body/eval_jaxpr/ap,bp->ab/dot_general | solution.py:22
  104.9 8.5 %copy.14 = f32[4,125,28,125]{1,3,2,0:T(8,128)} copy(f32[4,125,28,125]{3,1,2,0:T(8,128)} %fusion.19) | data formatting | bytes 14000000 | tf_op jit(solution)/shard_map/while/body/eval_jaxpr/ap,bp->ab/dot_general | solution.py:22
  113.4 6.3 %fusion.20 = f32[4]{0:T(128)S(1)} fusion(f32[4,125,28,125]{3,1,2,0:T(8,128)} %fusion.19, f32[4,125,28,125]{1,3,2,0:T(8,128)} %copy.14), kind=kLoop, calls=%fused_computation.1.clone.1 | loop fusion | flops 3499996 | bytes 14000016 | tf_op jit(solution)/shard_map/while/body/eval_jaxpr/reduce_sum | solution.py:30
  121.4 4.4 %reshape.56 = bf16[28,31250]{1,0:T(8,128)(2,1)S(1)} reshape(bf16[28,125,250]{2,1,0:T(8,128)(2,1)} %get-tuple-element.78) | data formatting | bytes 3500000 | tf_op jit(solution)/shard_map/while/body/eval_jaxpr/reshape | solution.py:19
  131.4 8.5 %copy.14 = f32[4,125,28,125]{1,3,2,0:T(8,128)} copy(f32[4,125,28,125]{3,1,2,0:T(8,128)} %fusion.19) | data formatting | bytes 14000000 | tf_op jit(solution)/shard_map/while/body/eval_jaxpr/ap,bp->ab/dot_general | solution.py:22
  139.9 6.3 %fusion.20 = f32[4]{0:T(128)S(1)} fusion(f32[4,125,28,125]{3,1,2,0:T(8,128)} %fusion.19, f32[4,125,28,125]{1,3,2,0:T(8,128)} %copy.14), kind=kLoop, calls=%fused_computation.1.clone.1 | loop fusion | flops 3499996 | bytes 14000016 | tf_op jit(solution)/shard_map/while/body/eval_jaxpr/reduce_sum | solution.py:30
  147.8 4.4 %reshape.56 = bf16[28,31250]{1,0:T(8,128)(2,1)S(1)} reshape(bf16[28,125,250]{2,1,0:T(8,128)(2,1)} %get-tuple-element.78) | data formatting | bytes 3500000 | tf_op jit(solution)/shard_map/while/body/eval_jaxpr/reshape | solution.py:19
  157.8 8.5 %copy.14 = f32[4,125,28,125]{1,3,2,0:T(8,128)} copy(f32[4,125,28,125]{3,1,2,0:T(8,128)} %fusion.19) | data formatting | bytes 14000000 | tf_op jit(solution)/shard_map/while/body/eval_jaxpr/ap,bp->ab/dot_general | solution.py:22
  166.4 6.3 %fusion.20 = f32[4]{0:T(128)S(1)} fusion(f32[4,125,28,125]{3,1,2,0:T(8,128)} %fusion.19, f32[4,125,28,125]{1,3,2,0:T(8,128)} %copy.14), kind=kLoop, calls=%fused_computation.1.clone.1 | loop fusion | flops 3499996 | bytes 14000016 | tf_op jit(solution)/shard_map/while/body/eval_jaxpr/reduce_sum | solution.py:30
  174.3 4.4 %reshape.56 = bf16[28,31250]{1,0:T(8,128)(2,1)S(1)} reshape(bf16[28,125,250]{2,1,0:T(8,128)(2,1)} %get-tuple-element.78) | data formatting | bytes 3500000 | tf_op jit(solution)/shard_map/while/body/eval_jaxpr/reshape | solution.py:19
  184.3 8.5 %copy.14 = f32[4,125,28,125]{1,3,2,0:T(8,128)} copy(f32[4,125,28,125]{3,1,2,0:T(8,128)} %fusion.19) | data formatting | bytes 14000000 | tf_op jit(solution)/shard_map/while/body/eval_jaxpr/ap,bp->ab/dot_general | solution.py:22
  192.8 6.3 %fusion.20 = f32[4]{0:T(128)S(1)} fusion(f32[4,125,28,125]{3,1,2,0:T(8,128)} %fusion.19, f32[4,125,28,125]{1,3,2,0:T(8,128)} %copy.14), kind=kLoop, calls=%fused_computation.1.clone.1 | loop fusion | flops 3499996 | bytes 14000016 | tf_op jit(solution)/shard_map/while/body/eval_jaxpr/reduce_sum | solution.py:30
  200.7 4.4 %reshape.56 = bf16[28,31250]{1,0:T(8,128)(2,1)S(1)} reshape(bf16[28,125,250]{2,1,0:T(8,128)(2,1)} %get-tuple-element.78) | data formatting | bytes 3500000 | tf_op jit(solution)/shard_map/while/body/eval_jaxpr/reshape | solution.py:19
  210.7 8.5 %copy.14 = f32[4,125,28,125]{1,3,2,0:T(8,128)} copy(f32[4,125,28,125]{3,1,2,0:T(8,128)} %fusion.19) | data formatting | bytes 14000000 | tf_op jit(solution)/shard_map/while/body/eval_jaxpr/ap,bp->ab/dot_general | solution.py:22
  219.3 6.3 %fusion.20 = f32[4]{0:T(128)S(1)} fusion(f32[4,125,28,125]{3,1,2,0:T(8,128)} %fusion.19, f32[4,125,28,125]{1,3,2,0:T(8,128)} %copy.14), kind=kLoop, calls=%fused_computation.1.clone.1 | loop fusion | flops 3499996 | bytes 14000016 | tf_op jit(solution)/shard_map/while/body/eval_jaxpr/reduce_sum | solution.py:30
  227.2 4.4 %reshape.56 = bf16[28,31250]{1,0:T(8,128)(2,1)S(1)} reshape(bf16[28,125,250]{2,1,0:T(8,128)(2,1)} %get-tuple-element.78) | data formatting | bytes 3500000 | tf_op jit(solution)/shard_map/while/body/eval_jaxpr/reshape | solution.py:19
  237.2 8.5 %copy.14 = f32[4,125,28,125]{1,3,2,0:T(8,128)} copy(f32[4,125,28,125]{3,1,2,0:T(8,128)} %fusion.19) | data formatting | bytes 14000000 | tf_op jit(solution)/shard_map/while/body/eval_jaxpr/ap,bp->ab/dot_general | solution.py:22
  245.7 6.3 %fusion.20 = f32[4]{0:T(128)S(1)} fusion(f32[4,125,28,125]{3,1,2,0:T(8,128)} %fusion.19, f32[4,125,28,125]{1,3,2,0:T(8,128)} %copy.14), kind=kLoop, calls=%fused_computation.1.clone.1 | loop fusion | flops 3499996 | bytes 14000016 | tf_op jit(solution)/shard_map/while/body/eval_jaxpr/reduce_sum | solution.py:30
  252.2 13.1 %all-reduce = f32[32]{0:T(128)S(1)} all-reduce(f32[32]{0:T(128)S(1)} %reshape.49), channel_id=2, replica_groups=mesh['gx'=4,'gy'=8] {'gy'}, use_global_device_ids=true, to_apply=%region_5.6.clone | all-reduce | flops 32 | bytes 256
  265.7 11.7 %psum.21 = f32[4]{0:T(128)S(1)} all-reduce(f32[4]{0:T(128)S(1)} %dynamic-slice.1), channel_id=1, replica_groups=mesh['gx'=4,'gy'=8] {'gx'}, use_global_device_ids=true, to_apply=%region_6.7 | all-reduce | flops 4 | bytes 32 | tf_op jit(solution)/shard_map/psum | solution.py:47
  278.6 12.4 %all-reduce.1 = (f32[]{:T(128)}, f32[]{:T(128)}) all-reduce(f32[]{:T(128)} %get-tuple-element.26, f32[]{:T(128)} %get-tuple-element.25), channel_id=1, replica_groups=mesh['gx'=4,'gy'=8] {'gy'}, use_global_device_ids=true, to_apply=%region_8.9 | all-reduce | flops 2 | bytes 16 | tf_op jit(solution)/shard_map/psum | solution.py:49
  (76 shorter events, 49.8 us)
Async XLA Ops:
  7.2 33.2 %all-gather.2.cloned.1.call-start = ((), (), s32[]{:S(2)}) async-start(), calls=%async_computation | async-start | bytes 2359296 | tf_op jit(solution)/shard_map/all_gather | solution.py:44
  40.4 224.9 %copy-start.1 = (bf16[4,125,250]{2,0,1:T(4,128)(2,1)S(1)}, bf16[4,125,250]{2,0,1:T(4,128)(2,1)}, u32[]{:S(2)}) copy-start(bf16[4,125,250]{2,0,1:T(4,128)(2,1)} %param.6) | copy-start | bytes 750004
  40.4 225.0 %copy-start.2 = (f32[125,250]{1,0:T(8,128)S(1)}, f32[125,250]{1,0:T(8,128)}, u32[]{:S(2)}) copy-start(f32[125,250]{1,0:T(8,128)} %param.8) | copy-start | bytes 375004
  40.4 237.0 %copy-start.3 = (f32[4]{0:T(128)S(1)}, f32[4]{0:T(128)}, u32[]{:S(2)}) copy-start(f32[4]{0:T(128)} %param.9) | copy-start | bytes 52
  46.3 1.5 copy-start
  72.8 1.5 copy-start
  99.3 1.5 copy-start
  125.7 1.5 copy-start
  152.2 1.5 copy-start
  178.6 1.5 copy-start
  205.1 1.5 copy-start
  231.6 1.5 copy-start
Sparse Core Ops, SparseCore 0:
  9.9 30.4 all-gather.1
where the time goes:
time: 302 us; the launch traced here: 300 us
  local copies, waits for them, and re-layouts  125 us (41%)
  other arithmetic  52.4 us (17%)
  matrix products  39 us (13%)
  blocking collectives  37.2 us (12%)
  waiting for transfers between devices  29.6 us (10%)
  between operations  17.1 us (6%)
    dot_general x8, local copies, waits for them, and re-layouts, pair_energy(): jnp.einsum('ap,bp->ab', green_block.reshape(walkers * occ, orb), vector_b...  68.3 us
    reduce_sum x8, other arithmetic, pair_energy(): jnp.sum(exchange * swapped, axis=(1, 2, 3))  50.8 us
    reshape x8, local copies, waits for them, and re-layouts, pair_energy(): vector_block.reshape(vectors, occ * orb)  34.9 us
    dot_general x8, matrix products, pair_energy(): jnp.einsum('ap,bp->ab', green_block.reshape(walkers * occ, orb), vector_b...  33.1 us
    all_gather x1, waiting for transfers between devices, shards(): lax.all_gather(greens, 'gy', axis=0, tiled=True)  29.6 us
    unnamed x1, blocking collectives  13.1 us
    psum x1, blocking collectives, shards(): lax.psum((jnp.sum(weights * local_energy), jnp.sum(weights)), 'gy')  12.4 us
    psum x1, blocking collectives, shards(): two_body = lax.psum(partial_value, 'gx')  11.7 us
  transfers between devices with their start and end apart: 1, of which 1 were waited for; matrix products, arithmetic and copies ran while one was open for 0% of the time, Pallas kernels for 0%

commit v1 on v0

v1 whole, which is shorter than its diff:
```python
import functools

import jax
import jax.numpy as jnp
from jax import lax
from jax.experimental import pallas as pl
from jax.experimental.pallas import tpu as pltpu
from jax.sharding import PartitionSpec as P

MESH = pl.DeviceIdType.MESH
LANE = 128


def up(value, unit):
    return -(-value // unit) * unit


def bits_of(mask):
    return [1 << b for b in range(mask.bit_length()) if mask >> b & 1]


def last_hop(mask, half):
    if mask & 1:
        return 1
    found = bits_of(mask)
    return found[-1] if half == 0 else found[0]


def depth_of(mask):
    return 2 * len(bits_of(mask & ~1)) + (mask & 1)


def arrival_steps(peers, halves):
    units = [(mask, half) for mask in range(peers) for half in range(halves)]
    if halves == 1:
        return [[unit] for unit in sorted(units, key=lambda u: (depth_of(u[0]), u[0]))]

    def rank(unit):
        mask, half = unit
        rest = mask & ~1
        late = 0
        if len(bits_of(rest)) == 1:
            late = (half + bits_of(rest)[0].bit_length()) % 2
        return (depth_of(mask), late, mask, half)

    units.sort(key=rank)
    return [units[i:i + 2] for i in range(0, len(units), 2)]


def kernel(ngx, ngy, greens_ref, chol_ref, body_ref, weight_ref, energy_ref, mean_ref,
           slots, gz, lp, lt, dga, dgb, rows, part, box_x, box_y, msg_x, msg_y,
           send_sem, recv_sem, xs_sem, xr_sem, ys_sem, yr_sem):
    gx = lax.axis_index("gx")
    gy = lax.axis_index("gy")
    wl, occ, orb = greens_ref.shape
    ng = chol_ref.shape[0]
    occ_p = lp.shape[0]
    tiles = lt.shape[1] // (2 * occ_p)
    halves = 2 if wl % 2 == 0 else 1
    hw = wl // halves

    def flip(mask):
        there = gy
        for bit in bits_of(mask):
            there = there + bit * (1 - 2 * ((there // bit) % 2))
        return there

    def x_peer(step):
        return (gx + step) % ngx

    barrier = pltpu.get_barrier_semaphore()
    for mask in range(1, ngy):
        pl.semaphore_signal(barrier, inc=1, device_id=(gx, flip(mask)), device_id_type=MESH)
    for step in range(1, ngx):
        pl.semaphore_signal(barrier, inc=1, device_id=(x_peer(step), gy), device_id_type=MESH)
    pl.semaphore_wait(barrier, ngy - 1 + ngx - 1)

    def hop(mask, half):
        over = last_hop(mask, half)
        before = mask ^ over
        span = pl.ds(half * hw, hw)
        source = greens_ref.at[span] if before == 0 else slots.at[before, span]
        return pltpu.make_async_remote_copy(
            src_ref=source, dst_ref=slots.at[mask, span],
            send_sem=send_sem.at[mask, half], recv_sem=recv_sem.at[mask, half],
            device_id=(gx, flip(over)), device_id_type=MESH)

    steps = arrival_steps(ngy, halves)
    order = [unit for step in steps for unit in step]

    def forward(unit):
        for mask, half in order:
            if mask and half == unit[1] and mask ^ last_hop(mask, half) == unit[0]:
                hop(mask, half).start()

    for half in range(halves):
        forward((0, half))

    gz[...] = jnp.zeros_like(gz)
    lp[...] = jnp.zeros_like(lp)
    for g in range(2 * tiles):
        if g < ng:
            lp[0:occ, 0:orb] = chol_ref[g]
            lt[:, g * occ_p:(g + 1) * occ_p] = lp[...].T
        else:
            lt[:, g * occ_p:(g + 1) * occ_p] = jnp.zeros((lt.shape[0], occ_p), lt.dtype)

    lane8 = lax.broadcasted_iota(jnp.int32, (8, occ_p), 1)
    sub8 = lax.broadcasted_iota(jnp.int32, (8, occ_p), 0)
    on_diag = (lane8 % 8) == sub8
    below = (lax.broadcasted_iota(jnp.int32, (occ_p, occ_p), 0)
             > lax.broadcasted_iota(jnp.int32, (occ_p, occ_p), 1))

    def diagonal(block):
        picked = block[0:8]
        for k in range(1, occ_p // 8):
            picked = jnp.where(lane8 >= 8 * k, block[8 * k:8 * k + 8], picked)
        return jnp.sum(jnp.where(on_diag, picked, 0.0), axis=0, keepdims=True)

    def step_body(s, carry):
        for at, units in enumerate(steps):
            @pl.when(s == at)
            def _():
                for unit in units:
                    if unit[0]:
                        hop(*unit).wait_recv()
                        forward(unit)
                for place, (mask, half) in enumerate(units):
                    for w in range(hw):
                        base = (place * hw + w) * occ_p
                        if mask:
                            gz[base:base + occ, 0:orb] = slots[mask, half * hw + w]
                        else:
                            gz[base:base + occ, 0:orb] = greens_ref[half * hw + w]

        totals = [jnp.zeros((8, occ_p), jnp.float32) for _ in range(wl)]
        for t in range(tiles):
            both = jnp.dot(gz[...], lt[:, t * 2 * occ_p:(t + 1) * 2 * occ_p],
                           preferred_element_type=jnp.float32)
            for w in range(wl):
                first = both[w * occ_p:(w + 1) * occ_p, 0:occ_p]
                second = both[w * occ_p:(w + 1) * occ_p, occ_p:2 * occ_p]
                mixed = jnp.where(below, first, second)
                other = jnp.where(below, second, first)
                product = other * mixed.T
                totals[w] = totals[w] + jnp.sum(product.reshape(occ_p // 8, 8, occ_p), axis=0)
                dga[w, t:t + 1, :] = diagonal(first)
                dgb[w, t:t + 1, :] = diagonal(second)
        for w in range(wl):
            da = dga[w]
            db = dgb[w]
            gap = da - db
            ca = jnp.sum(da, axis=1, keepdims=True)
            cb = jnp.sum(db, axis=1, keepdims=True)
            coulomb = jnp.sum(0.5 * (ca * ca + cb * cb), axis=0, keepdims=True)
            row = -jnp.sum(totals[w], axis=0, keepdims=True) - 0.5 * jnp.sum(gap * gap, axis=0, keepdims=True)
            rows[pl.ds(s, 1), w:w + 1, :] = jnp.where(lane8[0:1] == 0, row + coulomb, row).reshape(1, 1, occ_p)
        return carry

    lax.fori_loop(0, len(steps), step_body, 0)

    for s, units in enumerate(steps):
        for place, (mask, half) in enumerate(units):
            at = flip(mask) * wl + half * hw
            for w in range(hw):
                part[pl.ds(at + w, 1), :] = rows[s, place * hw + w:place * hw + w + 1, :]

    width = box_x.shape[2]
    walkers = ngy * wl
    summed = jnp.sum(part[...], axis=1, keepdims=True)
    spot = (lax.broadcasted_iota(jnp.int32, (walkers, width), 0)
            == lax.broadcasted_iota(jnp.int32, (walkers, width), 1))
    line = jnp.sum(jnp.where(spot, summed, 0.0), axis=0, keepdims=True)
    msg_x[...] = jnp.broadcast_to(line, msg_x.shape)
    box_x[pl.ds(gx, 1)] = jnp.broadcast_to(line, msg_x.shape)[None]

    def x_copy(step):
        return pltpu.make_async_remote_copy(
            src_ref=msg_x, dst_ref=box_x.at[gx], send_sem=xs_sem.at[step - 1],
            recv_sem=xr_sem.at[step - 1], device_id=(x_peer(step), gy), device_id_type=MESH)

    for step in range(1, ngx):
        x_copy(step).start()

    lane_w = lax.broadcasted_iota(jnp.int32, (8, width), 1)
    sub_w = lax.broadcasted_iota(jnp.int32, (8, width), 0)
    extra = jnp.zeros((8, width), jnp.float32)
    for w in range(wl):
        single = jnp.sum(greens_ref[w].astype(jnp.float32) * body_ref[...], axis=0, keepdims=True)
        single = jnp.sum(single, axis=1, keepdims=True)
        mine = lane_w == gy * wl + w
        extra = extra + jnp.where(mine & (sub_w == 0), single, 0.0)
        extra = extra + jnp.where(mine & (sub_w == 1), weight_ref[0:1, w:w + 1], 0.0)

    for step in range(1, ngx):
        x_copy(step).wait_recv()
    total = jnp.sum(box_x[...], axis=0)
    message = jnp.where(sub_w == 0, total, 0.0) + extra
    msg_y[...] = message
    box_y[pl.ds(gy, 1)] = message[None]

    def y_copy(mask):
        return pltpu.make_async_remote_copy(
            src_ref=msg_y, dst_ref=box_y.at[gy], send_sem=ys_sem.at[mask - 1],
            recv_sem=yr_sem.at[mask - 1], device_id=(gx, flip(mask)), device_id_type=MESH)

    for mask in range(1, ngy):
        y_copy(mask).start()
    for mask in range(1, ngy):
        y_copy(mask).wait_recv()
    final = jnp.sum(box_y[...], axis=0)
    energy = final[0:1]
    weight = final[1:2]
    mean = (jnp.sum(energy * weight, axis=1, keepdims=True)
            / jnp.sum(weight, axis=1, keepdims=True))
    for w in range(wl):
        energy_ref[0:1, w:w + 1] = jnp.sum(
            jnp.where(lane_w[0:1] == gy * wl + w, energy, 0.0), axis=1, keepdims=True)
    mean_ref[...] = mean

    for step in range(1, ngx):
        x_copy(step).wait_send()
    for mask in range(1, ngy):
        y_copy(mask).wait_send()
        for half in range(halves):
            hop(mask, half).wait_send()


def shards(ngx, ngy, greens, chol_rot, one_body, weights):
    wl, occ, orb = greens.shape
    ng = chol_rot.shape[0]
    occ_p, orb_p = up(occ, LANE), up(orb, 2 * LANE)
    tiles = up(ng, 2) // 2
    halves = 2 if wl % 2 == 0 else 1
    width = up(ngy * wl, LANE)
    vmem = pl.BlockSpec(memory_space=pltpu.VMEM)
    f32, bf16 = jnp.float32, jnp.bfloat16
    dma = pltpu.SemaphoreType.DMA
    energy, mean = pl.pallas_call(
        functools.partial(kernel, ngx, ngy),
        out_shape=(jax.ShapeDtypeStruct((1, wl), f32), jax.ShapeDtypeStruct((1, 1), f32)),
        in_specs=[vmem] * 4,
        out_specs=(vmem, vmem),
        scratch_shapes=[
            pltpu.VMEM((ngy, wl, occ, orb), bf16),
            pltpu.VMEM((wl * occ_p, orb_p), bf16),
            pltpu.VMEM((occ_p, orb_p), bf16),
            pltpu.VMEM((orb_p, 2 * tiles * occ_p), bf16),
            pltpu.VMEM((wl, tiles, occ_p), f32),
            pltpu.VMEM((wl, tiles, occ_p), f32),
            pltpu.VMEM((ngy, wl, occ_p), f32),
            pltpu.VMEM((ngy * wl, occ_p), f32),
            pltpu.VMEM((ngx, 8, width), f32),
            pltpu.VMEM((ngy, 8, width), f32),
            pltpu.VMEM((8, width), f32),
            pltpu.VMEM((8, width), f32),
            dma((ngy, halves)), dma((ngy, halves)),
            dma((max(ngx - 1, 1),)), dma((max(ngx - 1, 1),)),
            dma((max(ngy - 1, 1),)), dma((max(ngy - 1, 1),)),
        ],
        compiler_params=pltpu.CompilerParams(
            collective_id=0, has_side_effects=True, vmem_limit_bytes=48 * 2**20),
    )(greens, chol_rot, one_body, weights.reshape(1, wl))
    return energy.reshape(wl), mean.reshape(())


def solution(mesh):
    ngx, ngy = mesh.shape["gx"], mesh.shape["gy"]
    placed = (P("gy", None, None), P(("gx", "gy"), None, None), P(), P("gy"))
    return jax.shard_map(
        functools.partial(shards, ngx, ngy), mesh=mesh, in_specs=placed,
        out_specs=(P("gy"), P()), check_vma=False,
    )
```

time: 302 us -> 38.1 us (0.13)
  local copies, waits for them, and re-layouts: 125 us -> 4.54 us
  other arithmetic: 52.4 us -> 0 us
  matrix products: 39 us -> 0 us
  blocking collectives: 37.2 us -> 0 us
  Pallas kernels: 0 us -> 31 us
  waiting for transfers between devices: 29.6 us -> 0 us
  between operations: 17.1 us -> 2.39 us
    dot_general x8 -> x0, local copies, waits for them, and re-layouts: 68.3 us -> none  [pair_energy(): jnp.einsum('ap,bp->ab', green_block.reshape(walkers * occ, orb), vector_b...]
    reduce_sum x10 -> x0, other arithmetic: 52.3 us -> none  [the longest x8 50.8 us: pair_energy(): jnp.sum(exchange * swapped, axis=(1, 2, 3))]
    reshape x17 -> x0, local copies, waits for them, and re-layouts: 39.3 us -> none  [the longest x8 34.9 us: pair_energy(): vector_block.reshape(vectors, occ * orb)]
    dot_general x16 -> x0, matrix products: 39 us -> none  [the longest x8 33.1 us: pair_energy(): jnp.einsum('ap,bp->ab', green_block.reshape(walkers * occ, orb), vector_b...]
    pallas_call x0 -> x1, Pallas kernels: none -> 31 us  [shards(): pl.pallas_call(functools.partial(kernel, ngx, ngy), out_shape=(jax.ShapeD...]
    all_gather x1 -> x0, waiting for transfers between devices: 29.6 us -> none  [shards(): lax.all_gather(greens, 'gy', axis=0, tiled=True)]
    psum x2 -> x0, blocking collectives: 24.1 us -> none  [the longest x1 12.4 us: shards(): lax.psum((jnp.sum(weights * local_energy), jnp.sum(weights)), 'gy')]
    unnamed x1 -> x0, blocking collectives: 13.1 us -> none
  transfers between devices with their start and end apart: 1 -> 0, of which waited for: 1 -> 0; matrix products, arithmetic and copies ran while one was open for 0% -> 0% of each run, Pallas kernels for 0% -> 0%
where the time goes in v1:
time: 38.1 us; the launch traced here: 37.9 us
  Pallas kernels  31 us (81%)
  local copies, waits for them, and re-layouts  4.54 us (12%)
  between operations  2.39 us (6%)
    pallas_call x1, Pallas kernels, shards(): pl.pallas_call(functools.partial(kernel, ngx, ngy), out_shape=(jax.ShapeD...  31 us
    unnamed x8, local copies, waits for them, and re-layouts  4.54 us

profile of v1, /device:TPU:0, one launch (start us, length us, event | category | flops | bytes accessed | tf_op | source)
XLA Modules:
  0.0 37.9 jit_solution(6356612838693787845)
XLA Ops:
  0.6 1.0 %copy.6.greens_ref = bf16[4,125,250]{2,1,0:T(8,128)(2,1)S(1)} copy(bf16[4,125,250]{2,0,1:T(4,128)(2,1)} %param.4) | data formatting | bytes 500000 | tf_op args[0]
  1.6 0.0 copy-start
  1.6 1.5 %copy-done = bf16[28,125,250]{2,1,0:T(8,128)(2,1)S(1)} copy-done((bf16[28,125,250]{2,1,0:T(8,128)(2,1)S(1)}, bf16[28,125,250]{2,1,0:T(8,128)(2,1)}, u32[]{:S(2)}) %copy-start) | copy-done | bytes 1750024
  3.1 0.0 copy-start.1
  3.1 0.9 %copy-done.1 = f32[125,250]{1,0:T(8,128)S(1)} copy-done((f32[125,250]{1,0:T(8,128)S(1)}, f32[125,250]{1,0:T(8,128)}, u32[]{:S(2)}) %copy-start.1) | copy-done | bytes 125024
  4.0 0.0 copy-start.2
  4.0 0.7 %copy-done.2 = f32[4]{0:T(128)S(1)} copy-done((f32[4]{0:T(128)S(1)}, f32[4]{0:T(128)}, u32[]{:S(2)}) %copy-start.2) | copy-done | bytes 40
  4.7 31.0 %shard_map.59 = (f32[1,4]{1,0:T(1,128)S(1)}, f32[1,1]{1,0:T(1,128)}) custom-call(bf16[4,125,250]{2,1,0:T(8,128)(2,1)S(1)} %copy.6.greens_ref, bf16[28,125,250]{2,1,0:T(8,128)(2,1)S(1)} %copy-done, f32[125,250]{1,0:T(8,128)S(1)} %copy-done.1, f32[1,4]{1,0:T(1,128)S(1)} %bitcast.3), custom_call_target="tpu_custom_call" | custom-call | tf_op jit(solution)/shard_map/pallas_call | solution.py:239
  35.7 0.5 %copy.9 = f32[4]{0:T(128)} copy(f32[4]{0:T(128)S(1)} %bitcast.4) | data formatting | bytes 32
Async XLA Ops:
  1.6 1.5 %copy-start = (bf16[28,125,250]{2,1,0:T(8,128)(2,1)S(1)}, bf16[28,125,250]{2,1,0:T(8,128)(2,1)}, u32[]{:S(2)}) copy-start(bf16[28,125,250]{2,1,0:T(8,128)(2,1)} %chol_ref.1) | copy-start | bytes 5250004
  3.1 0.9 %copy-start.1 = (f32[125,250]{1,0:T(8,128)S(1)}, f32[125,250]{1,0:T(8,128)}, u32[]{:S(2)}) copy-start(f32[125,250]{1,0:T(8,128)} %body_ref.1) | copy-start | bytes 375004
  4.0 0.7 %copy-start.2 = (f32[4]{0:T(128)S(1)}, f32[4]{0:T(128)}, u32[]{:S(2)}) copy-start(f32[4]{0:T(128)} %param.7) | copy-start | bytes 52

commit v2 on v1

--- a/solution.py
+++ b/solution.py
@@ -47,9 +47,9 @@
     return [units[i:i + 2] for i in range(0, len(units), 2)]
 
 
-def kernel(ngx, ngy, greens_ref, chol_ref, body_ref, weight_ref, energy_ref, mean_ref,
-           slots, gz, lp, lt, dga, dgb, rows, part, box_x, box_y, msg_x, msg_y,
-           send_sem, recv_sem, xs_sem, xr_sem, ys_sem, yr_sem):
+def kernel(ngx, ngy, greens_ref, chol_hbm, body_hbm, weight_hbm, energy_ref, mean_ref,
+           chol_ref, body_ref, weight_ref, slots, gz, lp, lt, dga, dgb, rows, part, extra, box, msg,
+           send_sem, recv_sem, load_sem, out_sem, in_sem):
     gx = lax.axis_index("gx")
     gy = lax.axis_index("gy")
     wl, occ, orb = greens_ref.shape
@@ -69,11 +69,16 @@
         return (gx + step) % ngx
 
     barrier = pltpu.get_barrier_semaphore()
-    for mask in range(1, ngy):
+    hops = [1 << b for b in range((ngy - 1).bit_length())]
+    for mask in hops:
         pl.semaphore_signal(barrier, inc=1, device_id=(gx, flip(mask)), device_id_type=MESH)
     for step in range(1, ngx):
         pl.semaphore_signal(barrier, inc=1, device_id=(x_peer(step), gy), device_id_type=MESH)
-    pl.semaphore_wait(barrier, ngy - 1 + ngx - 1)
+    loads = [pltpu.make_async_copy(src, dst, load_sem.at[i]) for i, (src, dst) in enumerate(
+        ((chol_hbm, chol_ref), (body_hbm, body_ref), (weight_hbm, weight_ref)))]
+    for load in loads:
+        load.start()
+    pl.semaphore_wait(barrier, len(hops) + ngx - 1)
 
     def hop(mask, half):
         over = last_hop(mask, half)
@@ -98,12 +103,24 @@
 
     gz[...] = jnp.zeros_like(gz)
     lp[...] = jnp.zeros_like(lp)
+    loads[0].wait()
     for g in range(2 * tiles):
         if g < ng:
             lp[0:occ, 0:orb] = chol_ref[g]
             lt[:, g * occ_p:(g + 1) * occ_p] = lp[...].T
         else:
             lt[:, g * occ_p:(g + 1) * occ_p] = jnp.zeros((lt.shape[0], occ_p), lt.dtype)
+
+    loads[1].wait()
+    loads[2].wait()
+    lane_e = lax.broadcasted_iota(jnp.int32, extra.shape, 1)
+    own = jnp.zeros(extra.shape, jnp.float32)
+    for w in range(wl):
+        single = jnp.sum(greens_ref[w].astype(jnp.float32) * body_ref[...], axis=0, keepdims=True)
+        single = jnp.sum(single, axis=1, keepdims=True)
+        own = own + jnp.where(lane_e == gy * wl + w, single, 0.0)
+        own = own + jnp.where(lane_e == (ngy + gy) * wl + w, weight_ref[0:1, w:w + 1], 0.0)
+    extra[...] = own
 
     lane8 = lax.broadcasted_iota(jnp.int32, (8, occ_p), 1)
     sub8 = lax.broadcasted_iota(jnp.int32, (8, occ_p), 0)
@@ -165,63 +182,44 @@
             for w in range(hw):
                 part[pl.ds(at + w, 1), :] = rows[s, place * hw + w:place * hw + w + 1, :]
 
-    width = box_x.shape[2]
+    width = box.shape[2]
     walkers = ngy * wl
-    summed = jnp.sum(part[...], axis=1, keepdims=True)
-    spot = (lax.broadcasted_iota(jnp.int32, (walkers, width), 0)
-            == lax.broadcasted_iota(jnp.int32, (walkers, width), 1))
-    line = jnp.sum(jnp.where(spot, summed, 0.0), axis=0, keepdims=True)
-    msg_x[...] = jnp.broadcast_to(line, msg_x.shape)
-    box_x[pl.ds(gx, 1)] = jnp.broadcast_to(line, msg_x.shape)[None]
-
-    def x_copy(step):
+    line = jnp.sum(part[...], axis=1, keepdims=True)
+    row_at = lax.broadcasted_iota(jnp.int32, (walkers, width), 0)
+    lane_at = lax.broadcasted_iota(jnp.int32, (walkers, width), 1)
+    line = jnp.sum(jnp.where(row_at == lane_at, line, 0.0), axis=0, keepdims=True)
+    line = line + jnp.where(gx == 0, extra[...], 0.0)
+    msg[...] = line
+    place = gx * ngy + gy
+    box[pl.ds(place, 1)] = line[None]
+
+    def share(across, mask):
         return pltpu.make_async_remote_copy(
-            src_ref=msg_x, dst_ref=box_x.at[gx], send_sem=xs_sem.at[step - 1],
-            recv_sem=xr_sem.at[step - 1], device_id=(x_peer(step), gy), device_id_type=MESH)
-
-    for step in range(1, ngx):
-        x_copy(step).start()
-
-    lane_w = lax.broadcasted_iota(jnp.int32, (8, width), 1)
-    sub_w = lax.broadcasted_iota(jnp.int32, (8, width), 0)
-    extra = jnp.zeros((8, width), jnp.float32)
-    for w in range(wl):
-        single = jnp.sum(greens_ref[w].astype(jnp.float32) * body_ref[...], axis=0, keepdims=True)
-        single = jnp.sum(single, axis=1, keepdims=True)
-        mine = lane_w == gy * wl + w
-        extra = extra + jnp.where(mine & (sub_w == 0), single, 0.0)
-        extra = extra + jnp.where(mine & (sub_w == 1), weight_ref[0:1, w:w + 1], 0.0)
-
-    for step in range(1, ngx):
-        x_copy(step).wait_recv()
-    total = jnp.sum(box_x[...], axis=0)
-    message = jnp.where(sub_w == 0, total, 0.0) + extra
-    msg_y[...] = message
-    box_y[pl.ds(gy, 1)] = message[None]
-
-    def y_copy(mask):
-        return pltpu.make_async_remote_copy(
-            src_ref=msg_y, dst_ref=box_y.at[gy], send_sem=ys_sem.at[mask - 1],
-            recv_sem=yr_sem.at[mask - 1], device_id=(gx, flip(mask)), device_id_type=MESH)
-
-    for mask in range(1, ngy):
-        y_copy(mask).start()
-    for mask in range(1, ngy):
-        y_copy(mask).wait_recv()
-    final = jnp.sum(box_y[...], axis=0)
-    energy = final[0:1]
-    weight = final[1:2]
-    mean = (jnp.sum(energy * weight, axis=1, keepdims=True)
+            src_ref=msg, dst_ref=box.at[place], send_sem=out_sem.at[across, mask],
+            recv_sem=in_sem.at[across, mask], device_id=(x_peer(across), flip(mask)),
+            device_id_type=MESH)
+
+    others = [(across, mask) for across in range(ngx) for mask in range(ngy) if across or mask]
+    others.sort(key=lambda o: -(min(o[0], ngx - o[0]) + depth_of(o[1])))
+    for other in others:
+        share(*other).start()
+    for other in others:
+        share(*other).wait_recv()
+    final = jnp.sum(box[...], axis=0)
+    lane_1 = lane_at[0:1]
+    weight = jnp.where(lane_1 >= walkers, final, 0.0)
+    energy = jnp.where(lane_1 < walkers, final, 0.0)
+    shifted = pltpu.roll(energy, walkers, 1)
+    mean = (jnp.sum(shifted * weight, axis=1, keepdims=True)
             / jnp.sum(weight, axis=1, keepdims=True))
     for w in range(wl):
         energy_ref[0:1, w:w + 1] = jnp.sum(
-            jnp.where(lane_w[0:1] == gy * wl + w, energy, 0.0), axis=1, keepdims=True)
+            jnp.where(lane_1 == gy * wl + w, energy, 0.0), axis=1, keepdims=True)
     mean_ref[...] = mean
 
-    for step in range(1, ngx):
-        x_copy(step).wait_send()
+    for other in others:
+        share(*other).wait_send()
     for mask in range(1, ngy):
-        y_copy(mask).wait_send()
         for half in range(halves):
             hop(mask, half).wait_send()
 
@@ -232,16 +230,20 @@
     occ_p, orb_p = up(occ, LANE), up(orb, 2 * LANE)
     tiles = up(ng, 2) // 2
     halves = 2 if wl % 2 == 0 else 1
-    width = up(ngy * wl, LANE)
+    width = up(2 * ngy * wl, LANE)
     vmem = pl.BlockSpec(memory_space=pltpu.VMEM)
+    hbm = pl.BlockSpec(memory_space=pltpu.HBM)
     f32, bf16 = jnp.float32, jnp.bfloat16
     dma = pltpu.SemaphoreType.DMA
     energy, mean = pl.pallas_call(
         functools.partial(kernel, ngx, ngy),
         out_shape=(jax.ShapeDtypeStruct((1, wl), f32), jax.ShapeDtypeStruct((1, 1), f32)),
-        in_specs=[vmem] * 4,
+        in_specs=[vmem, hbm, hbm, hbm],
         out_specs=(vmem, vmem),
         scratch_shapes=[
+            pltpu.VMEM((ng, occ, orb), bf16),
+            pltpu.VMEM((occ, orb), f32),
+            pltpu.VMEM((1, wl), f32),
             pltpu.VMEM((ngy, wl, occ, orb), bf16),
             pltpu.VMEM((wl * occ_p, orb_p), bf16),
             pltpu.VMEM((occ_p, orb_p), bf16),
@@ -250,13 +252,11 @@
             pltpu.VMEM((wl, tiles, occ_p), f32),
             pltpu.VMEM((ngy, wl, occ_p), f32),
             pltpu.VMEM((ngy * wl, occ_p), f32),
-            pltpu.VMEM((ngx, 8, width), f32),
-            pltpu.VMEM((ngy, 8, width), f32),
-            pltpu.VMEM((8, width), f32),
-            pltpu.VMEM((8, width), f32),
+            pltpu.VMEM((1, width), f32),
+            pltpu.VMEM((ngx * ngy, 1, width), f32),
+            pltpu.VMEM((1, width), f32),
             dma((ngy, halves)), dma((ngy, halves)),
-            dma((max(ngx - 1, 1),)), dma((max(ngx - 1, 1),)),
-            dma((max(ngy - 1, 1),)), dma((max(ngy - 1, 1),)),
+            dma((3,)), dma((ngx, ngy)), dma((ngx, ngy)),
         ],
         compiler_params=pltpu.CompilerParams(
             collective_id=0, has_side_effects=True, vmem_limit_bytes=48 * 2**20),

time: 38.1 us -> 36.5 us (0.958)
  Pallas kernels: 31 us -> 29.3 us
    pallas_call x1, Pallas kernels: 31 us -> 29.3 us  [shards(): pl.pallas_call(functools.partial(kernel, ngx, ngy), out_shape=(jax.ShapeD...]
where the time goes in v2:
time: 36.5 us; the launch traced here: 36.3 us
  Pallas kernels  29.3 us (80%)
  local copies, waits for them, and re-layouts  4.54 us (12%)
  between operations  2.39 us (7%)
    pallas_call x1, Pallas kernels, shards(): pl.pallas_call(functools.partial(kernel, ngx, ngy), out_shape=(jax.ShapeD...  29.3 us
    unnamed x8, local copies, waits for them, and re-layouts  4.54 us

profile of v2, /device:TPU:0, one launch (start us, length us, event | category | flops | bytes accessed | tf_op | source)
XLA Modules:
  0.0 36.3 jit_solution(13474418579938606425)
XLA Ops:
  0.6 1.0 %copy.6.greens_ref = bf16[4,125,250]{2,1,0:T(8,128)(2,1)S(1)} copy(bf16[4,125,250]{2,0,1:T(4,128)(2,1)} %param.4) | data formatting | bytes 500000 | tf_op args[0]
  1.6 0.0 copy-start
  1.6 1.5 %copy-done = bf16[28,125,250]{2,1,0:T(8,128)(2,1)S(1)} copy-done((bf16[28,125,250]{2,1,0:T(8,128)(2,1)S(1)}, bf16[28,125,250]{2,1,0:T(8,128)(2,1)}, u32[]{:S(2)}) %copy-start) | copy-done | bytes 1750024
  3.1 0.0 copy-start.1
  3.1 0.9 %copy-done.1 = f32[125,250]{1,0:T(8,128)S(1)} copy-done((f32[125,250]{1,0:T(8,128)S(1)}, f32[125,250]{1,0:T(8,128)}, u32[]{:S(2)}) %copy-start.1) | copy-done | bytes 125024
  4.0 0.0 copy-start.2
  4.0 0.7 %copy-done.2 = f32[4]{0:T(128)S(1)} copy-done((f32[4]{0:T(128)S(1)}, f32[4]{0:T(128)}, u32[]{:S(2)}) %copy-start.2) | copy-done | bytes 40
  4.7 29.3 %shard_map.59 = (f32[1,4]{1,0:T(1,128)S(1)}, f32[1,1]{1,0:T(1,128)}) custom-call(bf16[4,125,250]{2,1,0:T(8,128)(2,1)S(1)} %copy.6.greens_ref, bf16[28,125,250]{2,1,0:T(8,128)(2,1)S(1)} %copy-done, f32[125,250]{1,0:T(8,128)S(1)} %copy-done.1, f32[1,4]{1,0:T(1,128)S(1)} %bitcast.3), custom_call_target="tpu_custom_call" | custom-call | tf_op jit(solution)/shard_map/pallas_call | solution.py:238
  34.0 0.5 %copy.9 = f32[4]{0:T(128)} copy(f32[4]{0:T(128)S(1)} %bitcast.4) | data formatting | bytes 32
Async XLA Ops:
  1.6 1.5 %copy-start = (bf16[28,125,250]{2,1,0:T(8,128)(2,1)S(1)}, bf16[28,125,250]{2,1,0:T(8,128)(2,1)}, u32[]{:S(2)}) copy-start(bf16[28,125,250]{2,1,0:T(8,128)(2,1)} %chol_hbm.1) | copy-start | bytes 5250004
  3.1 0.9 %copy-start.1 = (f32[125,250]{1,0:T(8,128)S(1)}, f32[125,250]{1,0:T(8,128)}, u32[]{:S(2)}) copy-start(f32[125,250]{1,0:T(8,128)} %body_hbm.1) | copy-start | bytes 375004
  4.0 0.7 %copy-start.2 = (f32[4]{0:T(128)S(1)}, f32[4]{0:T(128)}, u32[]{:S(2)}) copy-start(f32[4]{0:T(128)} %param.7) | copy-start | bytes 52

commit v3 on v2

--- a/solution.py
+++ b/solution.py
@@ -41,7 +41,7 @@
         late = 0
         if len(bits_of(rest)) == 1:
             late = (half + bits_of(rest)[0].bit_length()) % 2
-        return (depth_of(mask), late, mask, half)
+        return (len(bits_of(rest)), late, mask & 1, mask, half)
 
     units.sort(key=rank)
     return [units[i:i + 2] for i in range(0, len(units), 2)]
@@ -98,8 +98,9 @@
             if mask and half == unit[1] and mask ^ last_hop(mask, half) == unit[0]:
                 hop(mask, half).start()
 
-    for half in range(halves):
-        forward((0, half))
+    for mask, half in order:
+        if mask and mask == last_hop(mask, half):
+            hop(mask, half).start()
 
     gz[...] = jnp.zeros_like(gz)
     lp[...] = jnp.zeros_like(lp)
@@ -259,7 +260,7 @@
             dma((3,)), dma((ngx, ngy)), dma((ngx, ngy)),
         ],
         compiler_params=pltpu.CompilerParams(
-            collective_id=0, has_side_effects=True, vmem_limit_bytes=48 * 2**20),
+            collective_id=0, has_side_effects=True, vmem_limit_bytes=63 * 2**20),
     )(greens, chol_rot, one_body, weights.reshape(1, wl))
     return energy.reshape(wl), mean.reshape(())
 

time: 36.5 us -> 32.8 us (0.90)
  Pallas kernels: 29.3 us -> 27.5 us
  local copies, waits for them, and re-layouts: 4.54 us -> 2.8 us
    pallas_call x1, Pallas kernels: 29.3 us -> 27.5 us  [shards(): pl.pallas_call(functools.partial(kernel, ngx, ngy), out_shape=(jax.ShapeD...]
    unnamed x8 -> x2, local copies, waits for them, and re-layouts: 4.54 us -> 2.8 us
where the time goes in v3:
time: 32.8 us; the launch traced here: 32.6 us
  Pallas kernels  27.5 us (84%)
  local copies, waits for them, and re-layouts  2.8 us (9%)
  between operations  2.31 us (7%)
    pallas_call x1, Pallas kernels, shards(): pl.pallas_call(functools.partial(kernel, ngx, ngy), out_shape=(jax.ShapeD...  27.5 us
    unnamed x2, local copies, waits for them, and re-layouts  2.8 us

profile of v3, /device:TPU:0, one launch (start us, length us, event | category | flops | bytes accessed | tf_op | source)
XLA Modules:
  0.0 32.6 jit_solution(2015489737016856602)
XLA Ops:
  0.6 1.7 %copy.6.greens_ref = bf16[4,125,250]{2,1,0:T(8,128)(2,1)} copy(bf16[4,125,250]{2,0,1:T(4,128)(2,1)} %param.4) | data formatting | bytes 500000 | tf_op args[0]
  2.3 27.5 %shard_map.59 = (f32[1,4]{1,0:T(1,128)}, f32[1,1]{1,0:T(1,128)}) custom-call(bf16[4,125,250]{2,1,0:T(8,128)(2,1)} %copy.6.greens_ref, bf16[28,125,250]{2,1,0:T(8,128)(2,1)} %chol_hbm.1, f32[125,250]{1,0:T(8,128)} %body_hbm.1, f32[1,4]{1,0:T(1,128)} %bitcast.3), custom_call_target="tpu_custom_call" | custom-call | tf_op jit(solution)/shard_map/pallas_call | solution.py:239
  29.8 1.1 %copy.9 = f32[4]{0:T(128)} copy(f32[4]{0:T(128)} %bitcast.4) | data formatting | bytes 32
